TPU v7x, 32 devices: a whole 2x2x4 slice. The times are simulated.
32 devices in a mesh: zero: 2 (over core), cols: 4 (over y, x), ens: 4 (over z).
Axes of the slice: x: 2, y: 2, z: 4, core: 2. Of those that a mesh axis runs over, the one named last changes fastest.
Arguments:
- weight_gate: float32 [8192, 8192], P(('ens', 'zero'), 'cols'), parts along dimension 0, may hold values from -0.1875 to 0.1875
- moment_gate: float32 [8192, 8192], P(('ens', 'zero'), 'cols'), parts along dimension 0, may hold values from -0.125 to 0.125
- square_gate: float32 [8192, 8192], P(('ens', 'zero'), 'cols'), parts along dimension 0, may hold values from -0.125 to 0.125
- weight_up: float32 [8192, 8192], P(('ens', 'zero'), 'cols'), parts along dimension 0, may hold values from -0.1875 to 0.1875
- moment_up: float32 [8192, 8192], P(('ens', 'zero'), 'cols'), parts along dimension 0, may hold values from -0.125 to 0.125
- square_up: float32 [8192, 8192], P(('ens', 'zero'), 'cols'), parts along dimension 0, may hold values from -0.125 to 0.125
- norm_gain: float32 [8192], P(('ens', 'zero')), parts along dimension 0, may hold values from 0.25 to 1.75
Outputs:
- ready_gate: bfloat16 [8192, 8192], P('ens', 'cols'), parts along dimension 0
- ready_up: bfloat16 [8192, 8192], P('ens', 'cols'), parts along dimension 0
- factor_gate: float32 [32768], P(('ens', 'cols')), parts along dimension 0
- factor_up: float32 [32768], P(('ens', 'cols')), parts along dimension 0
There are 4 independent parts, one for each index of `ens`. A program takes and returns all parts, laid end to end along the dimension named above; each array names one. Nothing has to cross between parts.
All inputs are finite; a program needn't handle non-finite values. Where the computation divides by a largest or mean magnitude, that divisor is 1e-20 or more.
Results may differ from a plain program's by a relative error of at most 0.001.
Values may be sent and summed in bfloat16 or wider, within the bound.
No kernel may reach another device: no remote copies, remote signals or barrier semaphores. Data moves between devices by JAX's collectives and lax.ppermute only.
A program may use at most 128 MiB of HBM per device.

v0:
```python
import functools

import jax
import jax.numpy as jnp
from jax import lax
from jax.experimental import pallas as pl
from jax.experimental.pallas import tpu as pltpu
from jax.sharding import PartitionSpec as P


learn_rate = 0.2
hold_rate = 0.9
LANES = 128
BLOCKS = 16
ROWS = 16
GROUP = 512
AHEAD = 16
MIB = 2**20
VM = pl.BlockSpec(memory_space=pltpu.VMEM)
HB = pl.BlockSpec(memory_space=pltpu.HBM)

PARTS = {
    "x0": ((0, 0, 13),),
    "x1": ((0, 13, 3),),
    "b1": ((1, 0, 16),),
}
SENDS = {"b1": (10, 6)}
STEPS = (
    (("x0",), (), (), ()),
    (("x1", "b1"), (), (), ()),
    ((), ("b1",), (), ()),
    ((), (), ("b1.0", "b1.1"), ("x0",)),
    ((), (), (), ("x1", "b1.0")),
    ((), (), (), ("b1.1",)),
)


def sends(name):
    return [f"{name}.{k}" for k in range(len(SENDS[name]))]


def pieces(name, cols):
    unit = cols // 16
    part, _, k = name.partition(".")
    spans = PARTS[part]
    if k:
        skip, left, spans = sum(SENDS[part][: int(k)]), SENDS[part][int(k)], []
        for t, a, w in PARTS[part]:
            gone = min(skip, w)
            kept = min(left, w - gone)
            skip, left = skip - gone, left - kept
            if kept:
                spans.append((t, a + gone, kept))
    return [(t, a * unit, w * unit) for t, a, w in spans]


def width(name, cols):
    return sum(w for _, _, w in pieces(name, cols))


def blocks_of(rows):
    return min(BLOCKS, rows // ROWS)


def groups(w):
    return [(q, min(GROUP, w - q)) for q in range(0, w, GROUP)]


def loop(count, body, init):
    return lax.fori_loop(0, count, body, init, unroll=min(4, count))


def update_block(j, block, x, top, top_row, raw, first, rows, gain):
    for q, size in groups(x.shape[1]):
        lanes = pl.ds(q, size)
        wide = pl.ds(first + q, size)

        def body(i, high):
            r = pl.multiple_of(j * block + i * 8, 8)
            at = (pl.ds(r, 8), lanes)
            scale = jnp.concatenate([gain[pl.ds(r, 8), :]] * (size // LANES), axis=1)
            hold = hold_rate * raw[pl.ds(r, 8), wide] + raw[pl.ds(rows + r, 8), wide]
            value = (x[at] - learn_rate * hold) * scale
            x[at] = value
            return jnp.maximum(high, jnp.abs(value))

        top[pl.ds(top_row, 8), lanes] = loop(block // 8, body, top[pl.ds(top_row, 8), lanes])


def scale_block(j, block, source, side, inverse, target, first):
    for q, size in groups(target.shape[1]):
        lanes = pl.ds(q, size)
        wide = pl.ds(side + q, size)
        scale = jnp.broadcast_to(inverse[:, side + q : side + q + size], (16, size))

        def body(i, _):
            r = pl.multiple_of(j * block + i * 16, 16)
            target[pl.ds(first + r, 16), lanes] = (source[pl.ds(r, 16), wide] * scale).astype(target.dtype)
            return 0

        loop(block // 16, body, 0)


def step(n, rows, cols, plan, flags, *refs):
    new, scaled, owned, finished = plan
    opening, with_outs, fresh, last = flags
    refs = list(refs)

    def take(count):
        taken = refs[:count]
        del refs[:count]
        return taken

    count = blocks_of(rows)
    block = rows // count
    ahead = min(AHEAD, count)
    me = lax.axis_index("zero")
    used = sorted({t for name in new for t, _, _ in pieces(name, cols)})
    tensors = {t: take(3) for t in used}
    gain_in = take(1)[0] if new else None
    scale_in = {name: (take(1)[0], take(1)[0], take(n - 1)) for name in scaled}
    own_in = {name: take(1)[0] for name in owned}
    finish_in = {name: (take(1)[0] if name[0] == "x" else None, take(n - 1)) for name in finished}
    here_best = [name for name in scaled + finished if name in scaled or name[0] == "x"]
    past = [name for name in last if name not in here_best]
    old_best = dict(zip(past, take(len(past))))
    if with_outs and not fresh:
        take(2)
    gain = gain_in
    if opening:
        gain = take(1)[0]
    made = {name: take(1 if name[0] == "x" else 2) for name in new}
    owns = {name: take(len(SENDS[name])) for name in scaled}
    best = {name: take(1)[0] for name in here_best}
    outs = take(2) if with_outs else None
    fac_out = take(2) if last else None
    total = sum(width(name, cols) for name in new)
    if new:
        raw, load_sem = take(2)
    if opening:
        gain_row, gain_sem = take(2)
    stages = {name: take(1)[0] for name in finished if name[0] == "x"}
    if with_outs:
        out_sem = take(1)[0]
    if last:
        fac, fac_sem = take(2)

    if opening:
        fetch = pltpu.make_async_copy(gain_in, gain_row, gain_sem)
        fetch.start()
    spans = []
    first = 0
    for name in new:
        for t, c0, w in pieces(name, cols):
            if spans and spans[-1][0] == t and spans[-1][1] + spans[-1][2] == c0:
                spans[-1][2] += w
            else:
                spans.append([t, c0, w, first])
            first += w

    def load(j):
        here = pl.ds(j * block, block)
        for name in new:
            own = 0
            for t, c0, w in pieces(name, cols):
                target = made[name][0].at[here, pl.ds(own, w)]
                pltpu.make_async_copy(tensors[t][0].at[here, pl.ds(c0, w)], target, load_sem.at[j]).start()
                own += w
        for t, c0, w, side in spans:
            for k in range(2):
                target = raw.at[pl.ds(k * rows + j * block, block), pl.ds(side, w)]
                pltpu.make_async_copy(tensors[t][1 + k].at[here, pl.ds(c0, w)], target, load_sem.at[j]).start()

    if new:
        lax.fori_loop(0, ahead, lambda j, _: (load(j), 0)[1], 0)

    sem_at = 0
    waits = []

    def put(source, row, height, name, sem):
        at = 0
        for t, c0, w in pieces(name, cols):
            pltpu.make_async_copy(
                source.at[:, pl.ds(at, w)], outs[t].at[pl.ds(row, height), pl.ds(c0, w)], out_sem.at[sem]
            ).start()
            at += w

    for name in finished:
        if name[0] == "b":
            for k, other in enumerate(finish_in[name][1]):
                put(other, lax.rem(me + 1 + k, n) * rows, rows, name, sem_at)
                waits.append((other, sem_at))
                sem_at += 1
    for name in scaled:
        x, top, tops = scale_in[name]
        high = top[...]
        for other in tops:
            high = jnp.maximum(high, other[...])
        high = jnp.max(high, axis=0, keepdims=True)
        best[name][...] = jnp.broadcast_to(high, best[name].shape)
        inverse = 1.0 / high

        side = 0
        for target in owns[name]:

            def scale_own(j, _):
                scale_block(j, block, x, side, inverse, target, 0)
                return 0

            lax.fori_loop(0, count, scale_own, 0)
            side += target.shape[1]
    for name in owned:
        put(own_in[name], me * rows, rows, name, sem_at)
        waits.append((own_in[name], sem_at))
        sem_at += 1
    for name in finished:
        if name[0] == "x":
            own, got = finish_in[name]
            sources = [own] + got
            high = own[pl.ds(rows, 8), :]
            for other in got:
                high = jnp.maximum(high, other[pl.ds(rows, 8), :])
            high = jnp.max(high, axis=0, keepdims=True)
            best[name][...] = jnp.broadcast_to(high, best[name].shape)
            inverse = 1.0 / high
            stage = stages[name]
            for s, source in enumerate(sources):

                def scale_both(j, _):
                    scale_block(j, block, source, 0, inverse, stage, s * rows)
                    row = lax.rem(me + s, n) * rows + j * block
                    put(stage.at[pl.ds(s * rows + j * block, block), :], row, block, name, sem_at)
                    return 0

                lax.fori_loop(0, count, scale_both, 0)
            waits.append((stage, sem_at))
            sem_at += 1

    if opening:
        fetch.wait()

        def spread(j, _):
            gain[pl.ds(j * LANES, LANES), :] = jnp.broadcast_to(gain_row[pl.ds(j, 1), :], (LANES, LANES)).T
            return 0

        lax.fori_loop(0, rows // LANES, spread, 0)

    def one(j, _):
        whole = raw.at[pl.ds(0, 3 * block), :]
        pltpu.make_async_copy(whole, whole, load_sem.at[j]).wait()

        @pl.when(j + ahead < count)
        def _():
            load(j + ahead)

        first = 0
        for name in new:
            x = made[name][0]
            top, row = (x, rows) if name[0] == "x" else (made[name][1], 0)
            update_block(j, block, x, top, row, raw, first, rows, gain)
            first += width(name, cols)
        return 0

    if new:
        for name in new:
            top, row = (made[name][0], rows) if name[0] == "x" else (made[name][1], 0)
            top[pl.ds(row, 8), :] = jnp.zeros((8, top.shape[1]), jnp.float32)
        lax.fori_loop(0, count, one, 0)

    for name in last:
        high = best[name] if name in best else old_best[name]
        first = 0
        for t, c0, w in pieces(name, cols):
            for q in range(0, w, LANES):
                row = (c0 + q) // LANES
                fac[t, row : row + 1, :] = high[0:1, first + q : first + q + LANES]
            first += w
    if last:
        fac_copies = [pltpu.make_async_copy(fac.at[t], fac_out[t], fac_sem.at[t]) for t in range(2)]
        for copy in fac_copies:
            copy.start()
        for copy in fac_copies:
            copy.wait()
    for whole, sem in waits:
        pltpu.make_async_copy(whole, whole, out_sem.at[sem]).wait()


def per_device(n, weight_gate, moment_gate, square_gate, weight_up, moment_up, square_up, norm_gain):
    rows, cols = weight_gate.shape
    far = [
        pltpu.with_memory_space_constraint(v, pltpu.HBM)
        for v in (weight_gate, moment_gate, square_gate, weight_up, moment_up, square_up)
    ]
    gain = pltpu.with_memory_space_constraint(norm_gain.reshape(rows // LANES, LANES), pltpu.HBM)
    back = [[(i, (i - k) % n) for i in range(n)] for k in range(1, n)]
    outs = None
    own, top, tops, got, best = {}, {}, {}, {}, {}
    wide = {name: width(name, cols) for name in [*PARTS, *(v for k in SENDS for v in sends(k))]}

    def swap(value):
        return [lax.ppermute(value, "zero", pairs) for pairs in back]

    for s, (new, scaled, owned, finished) in enumerate(STEPS):
        opening = s == 0
        with_outs = bool(owned or finished)
        fresh = outs is None
        last = tuple(PARTS) if s == len(STEPS) - 1 else ()
        args, specs, shapes, scratch, aliases = [], [], [], [], {}

        def add(values, spec):
            args.extend(values)
            specs.extend([spec] * len(values))

        for t in sorted({t for name in new for t, _, _ in pieces(name, cols)}):
            add(far[3 * t : 3 * t + 3], HB)
        if new:
            add([gain], HB if opening else VM)
        for name in scaled:
            add([own[name], top[name]] + tops[name], VM)
        add([own[name] for name in owned], VM)
        for name in finished:
            add(([own[name]] if name[0] == "x" else []) + got[name], VM)
        made_here = [name for name in scaled + finished if name in scaled or name[0] == "x"]
        old_best = [name for name in last if name not in made_here]
        add([best[name] for name in old_best], VM)
        if opening:
            shapes.append(pltpu.VMEM((rows, LANES), jnp.float32))
        for name in new:
            if name[0] == "x":
                shapes.append(pltpu.VMEM((rows + 8, wide[name]), jnp.float32))
            else:
                shapes.append(pltpu.VMEM((rows, wide[name]), jnp.float32))
                shapes.append(pltpu.VMEM((8, wide[name]), jnp.float32))
        shapes += [pltpu.VMEM((rows, wide[send]), jnp.bfloat16) for name in scaled for send in sends(name)]
        shapes += [pltpu.VMEM((8, wide[name]), jnp.float32) for name in made_here]
        out_specs = [VM] * len(shapes)
        total = sum(wide[name] for name in new)
        room = 2
        if new:
            scratch += [pltpu.VMEM((2 * rows, total), jnp.float32), pltpu.SemaphoreType.DMA((blocks_of(rows),))]
            room += 2 * rows * total * 4 // MIB
        if opening:
            scratch += [pltpu.VMEM((rows // LANES, LANES), jnp.float32), pltpu.SemaphoreType.DMA]
        for name in finished:
            if name[0] == "x":
                scratch.append(pltpu.VMEM((n * rows, wide[name]), jnp.bfloat16))
                room += n * rows * wide[name] * 2 // MIB + 1
        if with_outs:
            count = len(owned) + sum(1 if name[0] == "x" else n - 1 for name in finished)
            scratch.append(pltpu.SemaphoreType.DMA((count,)))
            if not fresh:
                for q in range(2):
                    aliases[len(args) + q] = len(shapes) + q
                add(outs, HB)
            shapes += [jax.ShapeDtypeStruct((n * rows, cols), jnp.bfloat16)] * 2
            out_specs += [HB] * 2
        if last:
            shapes += [jax.ShapeDtypeStruct((cols // LANES, LANES), jnp.float32)] * 2
            out_specs += [HB] * 2
            scratch += [pltpu.VMEM((2, cols // LANES, LANES), jnp.float32), pltpu.SemaphoreType.DMA((2,))]
        result = list(
            pl.pallas_call(
                functools.partial(
                    step, n, rows, cols, (new, scaled, owned, finished), (opening, with_outs, fresh, last)
                ),
                out_shape=shapes,
                in_specs=specs,
                out_specs=out_specs,
                scratch_shapes=scratch,
                input_output_aliases=aliases,
                cost_estimate=pl.CostEstimate(flops=10**8, bytes_accessed=16 * MIB, transcendentals=0),
                compiler_params=pltpu.CompilerParams(vmem_limit_bytes=room * MIB),
            )(*args)
        )
        if opening:
            gain = result.pop(0)
        for name in new:
            own[name] = result.pop(0)
            if name[0] == "b":
                top[name] = result.pop(0)
                tops[name] = swap(top[name])
            else:
                got[name] = swap(own[name])
        for name in scaled:
            for send in sends(name):
                own[send] = result.pop(0)
                got[send] = swap(own[send])
        for name in made_here:
            best[name] = result.pop(0)
        if with_outs:
            outs = [result.pop(0), result.pop(0)]
    return (outs[0], outs[1], result[0].reshape(-1), result[1].reshape(-1))


def solution(mesh):
    def body(*values):
        return per_device(mesh.shape["zero"], *values)

    split = P(("ens", "zero"), "cols")
    return jax.shard_map(
        body,
        mesh=mesh,
        in_specs=(split,) * 6 + (P(("ens", "zero")),),
        out_specs=(P("ens", "cols"), P("ens", "cols"), P(("ens", "cols")), P(("ens", "cols"))),
        check_vma=False,
    )
```

profile of v0, /device:TPU:0, one launch (start us, length us, event | category | flops | bytes accessed | tf_op | source)
XLA Modules:
  0.0 31.1 jit_solution(209382097259218385)
XLA Ops:
  0.6 7.2 %shard_map.102 = (f32[1024,128]{1,0:T(8,128)S(1)}, f32[1032,1664]{1,0:T(8,128)S(1)}) custom-call(f32[1024,2048]{1,0:T(8,128)} %refs_0_.3, f32[1024,2048]{1,0:T(8,128)} %refs_1_.3, f32[1024,2048]{1,0:T(8,128)} %refs_2_.3, f32[8,128]{1,0:T(8,128)} %bitcast.3), custom_call_target="tpu_custom_call" | custom-call | flops 100000000 | bytes 16777216 | tf_op jit(solution)/shard_map/pallas_call | solution.py:362
  7.9 0.6 %collective-permute-start.2 = (f32[1032,1664]{1,0:T(8,128)S(1)}, f32[1032,1664]{1,0:T(8,128)S(1)}, u32[]{:S(2)}, u32[]{:S(2)}) collective-permute-start(f32[1032,1664]{1,0:T(8,128)S(1)} %get-tuple-element.27.refs_2_), channel_id=1, source_target_pairs={{0,16},{16,0},{1,17},{17,1},{2,18},{18,2},{3,19},{19,3},{4,20},{20... | collective-permute-start | bytes 20606984 | tf_op jit(solution)/shard_map/ppermute | solution.py:301
  8.4 10.0 %shard_map.103 = (f32[1032,384]{1,0:T(8,128)S(1)}, f32[1024,2048]{1,0:T(8,128)S(1)}, f32[8,2048]{1,0:T(8,128)S(1)}) custom-call(f32[1024,2048]{1,0:T(8,128)} %refs_0_.3, f32[1024,2048]{1,0:T(8,128)} %refs_1_.3, f32[1024,2048]{1,0:T(8,128)} %refs_2_.3, f32[1024,2048]{1,0:T(8,128)} %refs_3_.1, f32[1024,2048]{1,0:T(8,128)} %refs_4_.1, f32[1024,2048]{1,0:T(8,128)} %refs_5_.1, ...), custom_call_target="tpu_custom_call" | custom-call | flops 100000000 | bytes 16777216 | tf_op jit(solution)/shard_map/pallas_call | solution.py:362
  18.4 0.1 collective-permute-start
  18.5 1.2 %collective-permute-done.refs_2_ = f32[8,2048]{1,0:T(8,128)S(1)} collective-permute-done((f32[8,2048]{1,0:T(8,128)S(1)}, f32[8,2048]{1,0:T(8,128)S(1)}, u32[]{:S(2)}, u32[]{:S(2)}) %collective-permute-start) | collective-permute-done | bytes 65568 | tf_op jit(solution)/shard_map/ppermute | solution.py:301
  19.8 0.7 %shard_map.104 = (bf16[1024,1280]{1,0:T(8,128)(2,1)S(1)}, bf16[1024,768]{1,0:T(8,128)(2,1)S(1)}, f32[8,2048]{1,0:T(8,128)S(1)}) custom-call(f32[1024,2048]{1,0:T(8,128)S(1)} %get-tuple-element.23.refs_0_, f32[8,2048]{1,0:T(8,128)S(1)} %get-tuple-element.24.refs_1_, f32[8,2048]{1,0:T(8,128)S(1)} %collective-permute-done.refs_2_), custom_call_target="tpu_custom_call" | custom-call | flops 100000000 | bytes 16777216 | tf_op jit(solution)/shard_map/pallas_call | solution.py:362
  20.5 0.2 collective-permute-start.4
  20.7 0.4 %collective-permute-start.3 = (f32[1032,384]{1,0:T(8,128)S(1)}, f32[1032,384]{1,0:T(8,128)S(1)}, u32[]{:S(2)}, u32[]{:S(2)}) collective-permute-start(f32[1032,384]{1,0:T(8,128)S(1)} %get-tuple-element.29.refs_0_), channel_id=1, source_target_pairs={{0,16},{16,0},{1,17},{17,1},{2,18},{18,2},{3,19},{19,3},{4,20},{20... | collective-permute-start | bytes 4755464 | tf_op jit(solution)/shard_map/ppermute | solution.py:301
  21.0 0.2 collective-permute-start.1
  21.2 0.0 collective-permute-done.2.refs_3_
  21.2 4.1 %shard_map.105 = (f32[8,1664]{1,0:T(8,128)S(1)}, bf16[2048,2048]{1,0:T(8,128)(2,1)}, bf16[2048,2048]{1,0:T(8,128)(2,1)}) custom-call(bf16[1024,1280]{1,0:T(8,128)(2,1)S(1)} %get-tuple-element.26.refs_0_, bf16[1024,768]{1,0:T(8,128)(2,1)S(1)} %get-tuple-element.25.refs_1_, f32[1032,1664]{1,0:T(8,128)S(1)} %get-tuple-element.27.refs_2_, ...), custom_call_target="tpu_custom_call" | custom-call | flops 100000000 | bytes 16777216 | tf_op jit(solution)/shard_map/pallas_call | solution.py:362
  25.3 2.4 %collective-permute-done.3.refs_1_ = f32[1032,384]{1,0:T(8,128)S(1)} collective-permute-done((f32[1032,384]{1,0:T(8,128)S(1)}, f32[1032,384]{1,0:T(8,128)S(1)}, u32[]{:S(2)}, u32[]{:S(2)}) %collective-permute-start.3) | collective-permute-done | bytes 1585184 | tf_op jit(solution)/shard_map/ppermute | solution.py:301
  27.7 0.0 collective-permute-done.4.refs_2_
  27.7 2.0 %shard_map.106 = (f32[8,384]{1,0:T(8,128)S(1)}, bf16[2048,2048]{1,0:T(8,128)(2,1)}, bf16[2048,2048]{1,0:T(8,128)(2,1)}) custom-call(f32[1032,384]{1,0:T(8,128)S(1)} %get-tuple-element.29.refs_0_, f32[1032,384]{1,0:T(8,128)S(1)} %collective-permute-done.3.refs_1_, ...), custom_call_target="tpu_custom_call", output_to_operand_aliasing={{1}: (3, {}), {2}: (4, {})} | custom-call | flops 100000000 | bytes 16777216 | tf_op jit(solution)/shard_map/pallas_call | solution.py:362
  29.7 0.2 collective-permute-done.1.refs_0_
  29.9 1.2 %shard_map.107 = (bf16[2048,2048]{1,0:T(8,128)(2,1)}, bf16[2048,2048]{1,0:T(8,128)(2,1)}, f32[16,128]{1,0:T(8,128)}, f32[16,128]{1,0:T(8,128)}) custom-call(bf16[1024,768]{1,0:T(8,128)(2,1)S(1)} %collective-permute-done.1.refs_0_, f32[8,1664]{1,0:T(8,128)S(1)} %get-tuple-element.28.refs_1_, ...), custom_call_target="tpu_custom_call", output_to_operand_aliasing={{0}: (4, {}), {1}: (5, {})} | custom-call | flops 100000000 | bytes 16777216 | tf_op jit(solution)/shard_map/pallas_call | solution.py:362
Async XLA Ops:
  7.9 13.3 %collective-permute-start.2 = (f32[1032,1664]{1,0:T(8,128)S(1)}, f32[1032,1664]{1,0:T(8,128)S(1)}, u32[]{:S(2)}, u32[]{:S(2)}) collective-permute-start(f32[1032,1664]{1,0:T(8,128)S(1)} %get-tuple-element.27.refs_2_), channel_id=1, source_target_pairs={{0,16},{16,0},{1,17},{17,1},{2,18},{18,2},{3,19},{19,3},{4,20},{20... | collective-permute-start | bytes 20606984 | tf_op jit(solution)/shard_map/ppermute | solution.py:301
  18.4 1.3 %collective-permute-start = (f32[8,2048]{1,0:T(8,128)S(1)}, f32[8,2048]{1,0:T(8,128)S(1)}, u32[]{:S(2)}, u32[]{:S(2)}) collective-permute-start(f32[8,2048]{1,0:T(8,128)S(1)} %get-tuple-element.24.refs_1_), channel_id=1, source_target_pairs={{0,16},{16,0},{1,17},{17,1},{2,18},{18,2},{3,19},{19,3},{4,20},{20... | collective-permute-start | bytes 196616 | tf_op jit(solution)/shard_map/ppermute | solution.py:301
  20.5 7.2 %collective-permute-start.4 = (bf16[1024,1280]{1,0:T(8,128)(2,1)S(1)}, bf16[1024,1280]{1,0:T(8,128)(2,1)S(1)}, u32[]{:S(2)}, u32[]{:S(2)}) collective-permute-start(bf16[1024,1280]{1,0:T(8,128)(2,1)S(1)} %get-tuple-element.26.refs_0_), channel_id=1, source_target_pairs={{0,16},{16,0},{1,17},{17,1},{2,18},{18,2},{3,19},{19,3},{4,20},{20... | collective-permute-start | bytes 7864328 | tf_op jit(solution)/shard_map/ppermute | solution.py:301
  20.7 7.0 %collective-permute-start.3 = (f32[1032,384]{1,0:T(8,128)S(1)}, f32[1032,384]{1,0:T(8,128)S(1)}, u32[]{:S(2)}, u32[]{:S(2)}) collective-permute-start(f32[1032,384]{1,0:T(8,128)S(1)} %get-tuple-element.29.refs_0_), channel_id=1, source_target_pairs={{0,16},{16,0},{1,17},{17,1},{2,18},{18,2},{3,19},{19,3},{4,20},{20... | collective-permute-start | bytes 4755464 | tf_op jit(solution)/shard_map/ppermute | solution.py:301
  21.0 8.9 %collective-permute-start.1 = (bf16[1024,768]{1,0:T(8,128)(2,1)S(1)}, bf16[1024,768]{1,0:T(8,128)(2,1)S(1)}, u32[]{:S(2)}, u32[]{:S(2)}) collective-permute-start(bf16[1024,768]{1,0:T(8,128)(2,1)S(1)} %get-tuple-element.25.refs_1_), channel_id=1, source_target_pairs={{0,16},{16,0},{1,17},{17,1},{2,18},{18,2},{3,19},{19,3},{4,20},{20... | collective-permute-start | bytes 4718600 | tf_op jit(solution)/shard_map/ppermute | solution.py:301
where the time goes:
time: 31.5 us; the launch traced here: 31.1 us
  Pallas kernels  25.2 us (80%)
  waiting for transfers between devices  3.89 us (12%)
  starting transfers between devices  1.39 us (4%)
  between operations  0.68 us (2%)
    pallas_call x6, Pallas kernels, per_device(): pl.pallas_call(functools.partial(step, n, rows, cols, (new, scaled, owned...  25.2 us
    ppermute x5, waiting for transfers between devices, swap(): return [lax.ppermute(value, 'zero', pairs) for pairs in back]  3.89 us
    ppermute x5, starting transfers between devices, swap(): return [lax.ppermute(value, 'zero', pairs) for pairs in back]  1.39 us
  transfers between devices with their start and end apart: 5, of which 3 were waited for; matrix products, arithmetic and copies ran while one was open for 0% of the time, Pallas kernels for 54%

commit v1 on v0

--- a/solution.py
+++ b/solution.py
@@ -15,6 +15,7 @@
 ROWS = 16
 GROUP = 512
 AHEAD = 16
+NEAR = (5,)
 MIB = 2**20
 VM = pl.BlockSpec(memory_space=pltpu.VMEM)
 HB = pl.BlockSpec(memory_space=pltpu.HBM)
@@ -67,10 +68,10 @@
 
 
 def loop(count, body, init):
-    return lax.fori_loop(0, count, body, init, unroll=min(4, count))
-
-
-def update_block(j, block, x, top, top_row, raw, first, rows, gain):
+    return lax.fori_loop(0, count, body, init, unroll=min(8, count))
+
+
+def update_block(j, block, x, top, top_row, raw, first, rows, gain, near):
     for q, size in groups(x.shape[1]):
         lanes = pl.ds(q, size)
         wide = pl.ds(first + q, size)
@@ -79,7 +80,11 @@
             r = pl.multiple_of(j * block + i * 8, 8)
             at = (pl.ds(r, 8), lanes)
             scale = jnp.concatenate([gain[pl.ds(r, 8), :]] * (size // LANES), axis=1)
-            hold = hold_rate * raw[pl.ds(r, 8), wide] + raw[pl.ds(rows + r, 8), wide]
+            if near is None:
+                square = raw[pl.ds(rows + r, 8), wide]
+            else:
+                square = near[0][pl.ds(r, 8), pl.ds(near[1] + q, size)]
+            hold = hold_rate * raw[pl.ds(r, 8), wide] + square
             value = (x[at] - learn_rate * hold) * scale
             x[at] = value
             return jnp.maximum(high, jnp.abs(value))
@@ -168,6 +173,8 @@
                 own += w
         for t, c0, w, side in spans:
             for k in range(2):
+                if 3 * t + 1 + k in NEAR:
+                    continue
                 target = raw.at[pl.ds(k * rows + j * block, block), pl.ds(side, w)]
                 pltpu.make_async_copy(tensors[t][1 + k].at[here, pl.ds(c0, w)], target, load_sem.at[j]).start()
 
@@ -245,9 +252,19 @@
 
         lax.fori_loop(0, rows // LANES, spread, 0)
 
+    def near_of(name):
+        (t, c0, _), *more = pieces(name, cols)
+        if 3 * t + 2 not in NEAR:
+            return None
+        assert not more
+        return tensors[t][2], c0
+
     def one(j, _):
-        whole = raw.at[pl.ds(0, 3 * block), :]
-        pltpu.make_async_copy(whole, whole, load_sem.at[j]).wait()
+        near = sum(w for t, _, w, _ in spans if 3 * t + 2 in NEAR)
+        for wide, lines in ((total - near, 3 * block), (near, 2 * block)):
+            if wide:
+                whole = raw.at[pl.ds(0, lines), pl.ds(0, wide)]
+                pltpu.make_async_copy(whole, whole, load_sem.at[j]).wait()
 
         @pl.when(j + ahead < count)
         def _():
@@ -257,7 +274,7 @@
         for name in new:
             x = made[name][0]
             top, row = (x, rows) if name[0] == "x" else (made[name][1], 0)
-            update_block(j, block, x, top, row, raw, first, rows, gain)
+            update_block(j, block, x, top, row, raw, first, rows, gain, near_of(name))
             first += width(name, cols)
         return 0
 
@@ -288,8 +305,8 @@
 def per_device(n, weight_gate, moment_gate, square_gate, weight_up, moment_up, square_up, norm_gain):
     rows, cols = weight_gate.shape
     far = [
-        pltpu.with_memory_space_constraint(v, pltpu.HBM)
-        for v in (weight_gate, moment_gate, square_gate, weight_up, moment_up, square_up)
+        v if k in NEAR else pltpu.with_memory_space_constraint(v, pltpu.HBM)
+        for k, v in enumerate((weight_gate, moment_gate, square_gate, weight_up, moment_up, square_up))
     ]
     gain = pltpu.with_memory_space_constraint(norm_gain.reshape(rows // LANES, LANES), pltpu.HBM)
     back = [[(i, (i - k) % n) for i in range(n)] for k in range(1, n)]
@@ -312,7 +329,8 @@
             specs.extend([spec] * len(values))
 
         for t in sorted({t for name in new for t, _, _ in pieces(name, cols)}):
-            add(far[3 * t : 3 * t + 3], HB)
+            for k in range(3 * t, 3 * t + 3):
+                add([far[k]], VM if k in NEAR else HB)
         if new:
             add([gain], HB if opening else VM)
         for name in scaled:

time: 31.5 us -> 30.9 us (0.981)
  Pallas kernels: 25.2 us -> 22.8 us
  local copies, waits for them, and re-layouts: 0 us -> 1.43 us
  starting transfers between devices: 1.39 us -> 2.06 us
    pallas_call x6, Pallas kernels: 25.2 us -> 22.8 us  [per_device(): pl.pallas_call(functools.partial(step, n, rows, cols, (new, scaled, owned...]
    unnamed x0 -> x2, local copies, waits for them, and re-layouts: none -> 1.43 us
    ppermute x5, starting transfers between devices: 1.39 us -> 2.06 us  [swap(): return [lax.ppermute(value, 'zero', pairs) for pairs in back]]
  transfers between devices with their start and end apart: 5 -> 5, of which waited for: 3 -> 3; matrix products, arithmetic and copies ran while one was open for 0% -> 0% of each run, Pallas kernels for 54% -> 47%
where the time goes in v1:
time: 30.9 us; the launch traced here: 30.6 us
  Pallas kernels  22.8 us (74%)
  waiting for transfers between devices  3.61 us (12%)
  starting transfers between devices  2.06 us (7%)
  local copies, waits for them, and re-layouts  1.43 us (5%)
  between operations  0.68 us (2%)
    pallas_call x6, Pallas kernels, per_device(): pl.pallas_call(functools.partial(step, n, rows, cols, (new, scaled, owned...  22.8 us
    ppermute x5, waiting for transfers between devices, swap(): return [lax.ppermute(value, 'zero', pairs) for pairs in back]  3.61 us
    ppermute x5, starting transfers between devices, swap(): return [lax.ppermute(value, 'zero', pairs) for pairs in back]  2.06 us
    unnamed x2, local copies, waits for them, and re-layouts  1.43 us
  transfers between devices with their start and end apart: 5, of which 3 were waited for; matrix products, arithmetic and copies ran while one was open for 0% of the time, Pallas kernels for 47%

profile of v1, /device:TPU:0, one launch (start us, length us, event | category | flops | bytes accessed | tf_op | source)
XLA Modules:
  0.0 30.6 jit_solution(4900964098577107464)
XLA Ops:
  0.6 0.0 copy-start
  0.6 7.3 %shard_map.102 = (f32[1024,128]{1,0:T(8,128)S(1)}, f32[1032,1664]{1,0:T(8,128)S(1)}) custom-call(f32[1024,2048]{1,0:T(8,128)} %refs_0_.3, f32[1024,2048]{1,0:T(8,128)} %refs_1_.3, f32[1024,2048]{1,0:T(8,128)} %refs_2_.3, f32[8,128]{1,0:T(8,128)} %bitcast.3), custom_call_target="tpu_custom_call" | custom-call | flops 100000000 | bytes 16777216 | tf_op jit(solution)/shard_map/pallas_call | solution.py:380
  7.9 0.6 %collective-permute-start.2 = (f32[1032,1664]{1,0:T(8,128)S(1)}, f32[1032,1664]{1,0:T(8,128)S(1)}, u32[]{:S(2)}, u32[]{:S(2)}) collective-permute-start(f32[1032,1664]{1,0:T(8,128)S(1)} %get-tuple-element.27.refs_2_), channel_id=1, source_target_pairs={{0,16},{16,0},{1,17},{17,1},{2,18},{18,2},{3,19},{19,3},{4,20},{20... | collective-permute-start | bytes 20606984 | tf_op jit(solution)/shard_map/ppermute | solution.py:318
  8.5 1.4 %copy-done = f32[1024,2048]{1,0:T(8,128)S(1)} copy-done((f32[1024,2048]{1,0:T(8,128)S(1)}, f32[1024,2048]{1,0:T(8,128)}, u32[]{:S(2)}) %copy-start) | copy-done | bytes 8388632
  9.9 7.6 %shard_map.103 = (f32[1032,384]{1,0:T(8,128)S(1)}, f32[1024,2048]{1,0:T(8,128)S(1)}, f32[8,2048]{1,0:T(8,128)S(1)}) custom-call(f32[1024,2048]{1,0:T(8,128)} %refs_0_.3, f32[1024,2048]{1,0:T(8,128)} %refs_1_.3, f32[1024,2048]{1,0:T(8,128)} %refs_2_.3, f32[1024,2048]{1,0:T(8,128)} %refs_3_.1, f32[1024,2048]{1,0:T(8,128)} %refs_4_.1, ...), custom_call_target="tpu_custom_call" | custom-call | flops 100000000 | bytes 16777216 | tf_op jit(solution)/shard_map/pallas_call | solution.py:380
  17.5 0.6 %collective-permute-start = (f32[8,2048]{1,0:T(8,128)S(1)}, f32[8,2048]{1,0:T(8,128)S(1)}, u32[]{:S(2)}, u32[]{:S(2)}) collective-permute-start(f32[8,2048]{1,0:T(8,128)S(1)} %get-tuple-element.24.refs_1_), channel_id=1, source_target_pairs={{0,16},{16,0},{1,17},{17,1},{2,18},{18,2},{3,19},{19,3},{4,20},{20... | collective-permute-start | bytes 196616 | tf_op jit(solution)/shard_map/ppermute | solution.py:318
  18.1 1.2 %collective-permute-done.refs_2_ = f32[8,2048]{1,0:T(8,128)S(1)} collective-permute-done((f32[8,2048]{1,0:T(8,128)S(1)}, f32[8,2048]{1,0:T(8,128)S(1)}, u32[]{:S(2)}, u32[]{:S(2)}) %collective-permute-start) | collective-permute-done | bytes 65568 | tf_op jit(solution)/shard_map/ppermute | solution.py:318
  19.2 0.7 %shard_map.104 = (bf16[1024,1280]{1,0:T(8,128)(2,1)S(1)}, bf16[1024,768]{1,0:T(8,128)(2,1)S(1)}, f32[8,2048]{1,0:T(8,128)S(1)}) custom-call(f32[1024,2048]{1,0:T(8,128)S(1)} %get-tuple-element.23.refs_0_, f32[8,2048]{1,0:T(8,128)S(1)} %get-tuple-element.24.refs_1_, f32[8,2048]{1,0:T(8,128)S(1)} %collective-permute-done.refs_2_), custom_call_target="tpu_custom_call" | custom-call | flops 100000000 | bytes 16777216 | tf_op jit(solution)/shard_map/pallas_call | solution.py:380
  19.9 0.4 %collective-permute-start.4 = (bf16[1024,1280]{1,0:T(8,128)(2,1)S(1)}, bf16[1024,1280]{1,0:T(8,128)(2,1)S(1)}, u32[]{:S(2)}, u32[]{:S(2)}) collective-permute-start(bf16[1024,1280]{1,0:T(8,128)(2,1)S(1)} %get-tuple-element.26.refs_0_), channel_id=1, source_target_pairs={{0,16},{16,0},{1,17},{17,1},{2,18},{18,2},{3,19},{19,3},{4,20},{20... | collective-permute-start | bytes 7864328 | tf_op jit(solution)/shard_map/ppermute | solution.py:318
  20.3 0.1 collective-permute-start.3
  20.5 0.4 %collective-permute-start.1 = (bf16[1024,768]{1,0:T(8,128)(2,1)S(1)}, bf16[1024,768]{1,0:T(8,128)(2,1)S(1)}, u32[]{:S(2)}, u32[]{:S(2)}) collective-permute-start(bf16[1024,768]{1,0:T(8,128)(2,1)S(1)} %get-tuple-element.25.refs_1_), channel_id=1, source_target_pairs={{0,16},{16,0},{1,17},{17,1},{2,18},{18,2},{3,19},{19,3},{4,20},{20... | collective-permute-start | bytes 4718600 | tf_op jit(solution)/shard_map/ppermute | solution.py:318
  20.9 0.0 collective-permute-done.2.refs_3_
  20.9 4.1 %shard_map.105 = (f32[8,1664]{1,0:T(8,128)S(1)}, bf16[2048,2048]{1,0:T(8,128)(2,1)}, bf16[2048,2048]{1,0:T(8,128)(2,1)}) custom-call(bf16[1024,1280]{1,0:T(8,128)(2,1)S(1)} %get-tuple-element.26.refs_0_, bf16[1024,768]{1,0:T(8,128)(2,1)S(1)} %get-tuple-element.25.refs_1_, f32[1032,1664]{1,0:T(8,128)S(1)} %get-tuple-element.27.refs_2_, ...), custom_call_target="tpu_custom_call" | custom-call | flops 100000000 | bytes 16777216 | tf_op jit(solution)/shard_map/pallas_call | solution.py:380
  24.9 2.2 %collective-permute-done.3.refs_1_ = f32[1032,384]{1,0:T(8,128)S(1)} collective-permute-done((f32[1032,384]{1,0:T(8,128)S(1)}, f32[1032,384]{1,0:T(8,128)S(1)}, u32[]{:S(2)}, u32[]{:S(2)}) %collective-permute-start.3) | collective-permute-done | bytes 1585184 | tf_op jit(solution)/shard_map/ppermute | solution.py:318
  27.1 0.0 collective-permute-done.4.refs_2_
  27.2 2.0 %shard_map.106 = (f32[8,384]{1,0:T(8,128)S(1)}, bf16[2048,2048]{1,0:T(8,128)(2,1)}, bf16[2048,2048]{1,0:T(8,128)(2,1)}) custom-call(f32[1032,384]{1,0:T(8,128)S(1)} %get-tuple-element.29.refs_0_, f32[1032,384]{1,0:T(8,128)S(1)} %collective-permute-done.3.refs_1_, ...), custom_call_target="tpu_custom_call", output_to_operand_aliasing={{1}: (3, {}), {2}: (4, {})} | custom-call | flops 100000000 | bytes 16777216 | tf_op jit(solution)/shard_map/pallas_call | solution.py:380
  29.2 0.2 collective-permute-done.1.refs_0_
  29.4 1.2 %shard_map.107 = (bf16[2048,2048]{1,0:T(8,128)(2,1)}, bf16[2048,2048]{1,0:T(8,128)(2,1)}, f32[16,128]{1,0:T(8,128)}, f32[16,128]{1,0:T(8,128)}) custom-call(bf16[1024,768]{1,0:T(8,128)(2,1)S(1)} %collective-permute-done.1.refs_0_, f32[8,1664]{1,0:T(8,128)S(1)} %get-tuple-element.28.refs_1_, ...), custom_call_target="tpu_custom_call", output_to_operand_aliasing={{0}: (4, {}), {1}: (5, {})} | custom-call | flops 100000000 | bytes 16777216 | tf_op jit(solution)/shard_map/pallas_call | solution.py:380
Async XLA Ops:
  0.6 9.3 %copy-start = (f32[1024,2048]{1,0:T(8,128)S(1)}, f32[1024,2048]{1,0:T(8,128)}, u32[]{:S(2)}) copy-start(f32[1024,2048]{1,0:T(8,128)} %refs_5_.1) | copy-start | bytes 25165828
  7.9 12.9 %collective-permute-start.2 = (f32[1032,1664]{1,0:T(8,128)S(1)}, f32[1032,1664]{1,0:T(8,128)S(1)}, u32[]{:S(2)}, u32[]{:S(2)}) collective-permute-start(f32[1032,1664]{1,0:T(8,128)S(1)} %get-tuple-element.27.refs_2_), channel_id=1, source_target_pairs={{0,16},{16,0},{1,17},{17,1},{2,18},{18,2},{3,19},{19,3},{4,20},{20... | collective-permute-start | bytes 20606984 | tf_op jit(solution)/shard_map/ppermute | solution.py:318
  17.5 1.7 %collective-permute-start = (f32[8,2048]{1,0:T(8,128)S(1)}, f32[8,2048]{1,0:T(8,128)S(1)}, u32[]{:S(2)}, u32[]{:S(2)}) collective-permute-start(f32[8,2048]{1,0:T(8,128)S(1)} %get-tuple-element.24.refs_1_), channel_id=1, source_target_pairs={{0,16},{16,0},{1,17},{17,1},{2,18},{18,2},{3,19},{19,3},{4,20},{20... | collective-permute-start | bytes 196616 | tf_op jit(solution)/shard_map/ppermute | solution.py:318
  19.9 7.2 %collective-permute-start.4 = (bf16[1024,1280]{1,0:T(8,128)(2,1)S(1)}, bf16[1024,1280]{1,0:T(8,128)(2,1)S(1)}, u32[]{:S(2)}, u32[]{:S(2)}) collective-permute-start(bf16[1024,1280]{1,0:T(8,128)(2,1)S(1)} %get-tuple-element.26.refs_0_), channel_id=1, source_target_pairs={{0,16},{16,0},{1,17},{17,1},{2,18},{18,2},{3,19},{19,3},{4,20},{20... | collective-permute-start | bytes 7864328 | tf_op jit(solution)/shard_map/ppermute | solution.py:318
  20.3 6.8 %collective-permute-start.3 = (f32[1032,384]{1,0:T(8,128)S(1)}, f32[1032,384]{1,0:T(8,128)S(1)}, u32[]{:S(2)}, u32[]{:S(2)}) collective-permute-start(f32[1032,384]{1,0:T(8,128)S(1)} %get-tuple-element.29.refs_0_), channel_id=1, source_target_pairs={{0,16},{16,0},{1,17},{17,1},{2,18},{18,2},{3,19},{19,3},{4,20},{20... | collective-permute-start | bytes 4755464 | tf_op jit(solution)/shard_map/ppermute | solution.py:318
  20.5 8.9 %collective-permute-start.1 = (bf16[1024,768]{1,0:T(8,128)(2,1)S(1)}, bf16[1024,768]{1,0:T(8,128)(2,1)S(1)}, u32[]{:S(2)}, u32[]{:S(2)}) collective-permute-start(bf16[1024,768]{1,0:T(8,128)(2,1)S(1)} %get-tuple-element.25.refs_1_), channel_id=1, source_target_pairs={{0,16},{16,0},{1,17},{17,1},{2,18},{18,2},{3,19},{19,3},{4,20},{20... | collective-permute-start | bytes 4718600 | tf_op jit(solution)/shard_map/ppermute | solution.py:318
